TPU v7x, 32 devices: a whole 2x2x4 slice. The times are simulated.
32 devices in a mesh: rep: 2 (over x), lev: 4 (over z), tile: 4 (over y, core).
Axes of the slice: x: 2, y: 2, z: 4, core: 2. Of those that a mesh axis runs over, the one named last changes fastest.
Arguments:
- tokens: bfloat16 [2, 8, 4, 8, 8, 768], P('rep', 'lev', 'tile'), may hold values from -6 to 6
- w_qkv: bfloat16 [768, 2304], P('tile'), may hold values from -0.21875 to 0.21875
- w_proj: bfloat16 [768, 768], P('tile'), may hold values from -0.21875 to 0.21875
- seam_codes: int32 [4, 2], replicated, may hold values from 0 to 1
- upstream: bfloat16 [2, 8, 4, 8, 8, 768], P('rep', 'lev', 'tile'), may hold values from -6 to 6
Outputs:
- output: bfloat16 [2, 8, 4, 8, 8, 768], P('rep', 'lev', 'tile')
- grad_tokens: bfloat16 [2, 8, 4, 8, 8, 768], P('rep', 'lev', 'tile')
- grad_qkv: float32 [768, 2304], P('tile')
- grad_proj: float32 [768, 768], P('tile')
Inputs may be any that keep to these rules, and one draw needn't show every extreme that they name: The tiles form a periodic grid of four rows of 1 tiles: tile t's eastern neighbour is (t + 1) mod 4 and its northern neighbour (t + 1) mod 4. seam_codes[t, 0] is 1 where the seam to the eastern neighbour runs reversed, seam_codes[t, 1] likewise for the northern neighbour.
All inputs are finite; a program needn't handle non-finite values.
Results may differ from a plain program's by a relative error of at most 0.019.
Values may be sent and summed in bfloat16 or wider, within the bound.
No kernel may reach another device: no remote copies, remote signals or barrier semaphores. Data moves between devices by JAX's collectives and lax.ppermute only.
A program may use at most 64 MiB of HBM per device.

v0:
```python
import jax
import jax.numpy as jnp
from jax import lax
from jax.sharding import PartitionSpec as P

HEAD_DIM = 32
WIN = 8
WIN_LEV = 2
EPSILON = 1e-05


def shifted(value, axis, steps):
    count = lax.axis_size(axis)
    pairs = [(source, (source + steps) % count) for source in range(count)]
    return lax.ppermute(value, axis, pairs)


def layer_stats(token_rows):
    values = token_rows.astype(jnp.float32)
    center = jnp.mean(values, axis=1, keepdims=True)
    spread = jnp.mean(jnp.square(values - center), axis=1, keepdims=True)
    inverse = lax.rsqrt(spread + EPSILON)
    return ((values - center) * inverse, inverse)


def norm_backward(upstream_rows, grad_hidden, normalized, inverse):
    centre = jnp.mean(grad_hidden, axis=1, keepdims=True)
    projected = jnp.mean(grad_hidden * normalized, axis=1, keepdims=True)
    total_grad = (
        upstream_rows.astype(jnp.float32)
        + (grad_hidden - centre - normalized * projected) * inverse
    )
    return total_grad.astype(jnp.bfloat16)


def roll_local(grid_field, east_flag, north_flag, north_step):
    shift_cells = WIN // 2
    east_part = shifted(grid_field[:, :, :shift_cells], "tile", -1)
    east_part = jnp.where(east_flag, east_part[:, ::-1], east_part)
    across = jnp.concatenate([grid_field[:, :, shift_cells:], east_part], axis=2)
    north_part = shifted(across[:, :shift_cells], "tile", -north_step)
    north_part = jnp.where(north_flag, north_part[:, :, ::-1], north_part)
    upward = jnp.concatenate([across[:, shift_cells:], north_part], axis=1)
    level_part = shifted(upward[:1], "lev", -1)
    return jnp.concatenate([upward[1:], level_part], axis=0)


def unroll_local(rolled, east_flag, north_flag, north_step):
    shift_cells = WIN // 2
    extent = rolled.shape[1]
    level_part = shifted(rolled[-1:], "lev", 1)
    upward = jnp.concatenate([level_part, rolled[:-1]], axis=0)
    north_part = upward[:, extent - shift_cells :]
    north_part = jnp.where(north_flag, north_part[:, :, ::-1], north_part)
    north_part = shifted(north_part, "tile", north_step)
    across = jnp.concatenate([north_part, upward[:, : extent - shift_cells]], axis=1)
    east_part = across[:, :, extent - shift_cells :]
    east_part = jnp.where(east_flag, east_part[:, ::-1], east_part)
    east_part = shifted(east_part, "tile", 1)
    return jnp.concatenate([east_part, across[:, :, : extent - shift_cells]], axis=2)


def to_windows(grid_field):
    levels = grid_field.shape[0]
    extent = grid_field.shape[1]
    channels = grid_field.shape[3]
    blocks = grid_field.reshape(
        levels // WIN_LEV, WIN_LEV, extent // WIN, WIN, extent // WIN, WIN, channels
    )
    blocks = blocks.transpose(0, 2, 4, 1, 3, 5, 6)
    return blocks.reshape(-1, WIN_LEV * WIN * WIN, channels)


def from_windows(windows, levels, extent):
    channels = windows.shape[-1]
    blocks = windows.reshape(
        levels // WIN_LEV, extent // WIN, extent // WIN, WIN_LEV, WIN, WIN, channels
    )
    blocks = blocks.transpose(0, 3, 1, 4, 2, 5, 6)
    return blocks.reshape(levels, extent, extent, channels)


def split_heads(packed):
    windows = packed.shape[0]
    tokens = packed.shape[1]
    model_width = packed.shape[2] // 3
    head_count = model_width // HEAD_DIM
    query_part = packed[:, :, :model_width].reshape(windows, tokens, head_count, HEAD_DIM)
    key_part = packed[:, :, model_width : 2 * model_width].reshape(
        windows, tokens, head_count, HEAD_DIM
    )
    value_part = packed[:, :, 2 * model_width :].reshape(windows, tokens, head_count, HEAD_DIM)
    return (query_part, key_part, value_part)


def window_mask(wrap_flags, tokens):
    level_of = jnp.arange(tokens, dtype=jnp.int32) // (WIN * WIN)
    same_level = level_of[:, None] == level_of[None, :]
    allowed = jnp.logical_or(
        same_level[None, None], jnp.logical_not(wrap_flags)[:, None, None, None]
    )
    return allowed.astype(jnp.float32)


def attend_forward(packed, wrap_flags):
    query_part, key_part, value_part = split_heads(packed)
    scores = jnp.einsum(
        "wqhd,wkhd->whqk", query_part, key_part, preferred_element_type=jnp.float32
    ) * HEAD_DIM ** (-0.5)
    raised = jnp.exp(scores) * window_mask(wrap_flags, packed.shape[1])
    prob = raised / jnp.sum(raised, axis=-1, keepdims=True)
    prob_low = prob.astype(jnp.bfloat16)
    attended = jnp.einsum(
        "whqk,wkhd->wqhd", prob_low, value_part, preferred_element_type=jnp.float32
    )
    attended = attended.astype(jnp.bfloat16).reshape(packed.shape[0], packed.shape[1], -1)
    return (attended, prob, prob_low)


def attend_backward(packed, back_windows, prob, prob_low):
    query_part, key_part, value_part = split_heads(packed)
    back_heads = back_windows.reshape(query_part.shape)
    grad_value = jnp.einsum(
        "whqk,wqhd->wkhd", prob_low, back_heads, preferred_element_type=jnp.float32
    )
    grad_prob = jnp.einsum(
        "wqhd,wkhd->whqk", back_heads, value_part, preferred_element_type=jnp.float32
    )
    centre = jnp.sum(prob * grad_prob, axis=-1, keepdims=True)
    grad_scores = (prob * (grad_prob - centre) * HEAD_DIM ** (-0.5)).astype(jnp.bfloat16)
    grad_query = jnp.einsum(
        "whqk,wkhd->wqhd", grad_scores, key_part, preferred_element_type=jnp.float32
    )
    grad_key = jnp.einsum(
        "whqk,wqhd->wkhd", grad_scores, query_part, preferred_element_type=jnp.float32
    )
    windows = packed.shape[0]
    tokens = packed.shape[1]
    joined = jnp.concatenate(
        [
            grad_query.reshape(windows, tokens, -1),
            grad_key.reshape(windows, tokens, -1),
            grad_value.reshape(windows, tokens, -1),
        ],
        axis=-1,
    )
    return joined.astype(jnp.bfloat16)


def shards(tokens, w_qkv, w_proj, seam_codes, upstream):
    levels = tokens.shape[1]
    extent = tokens.shape[3]
    model_width = tokens.shape[5]
    tiles_count = lax.axis_size("tile")
    north_step = tiles_count // 4
    tile_here = lax.axis_index("tile")
    east_flag = seam_codes[tile_here, 0] == 1
    north_flag = seam_codes[tile_here, 1] == 1
    top_level = lax.axis_index("lev") == lax.axis_size("lev") - 1
    per_level = extent // WIN * (extent // WIN)
    window_total = levels // WIN_LEV * per_level
    lev_window = jnp.arange(window_total, dtype=jnp.int32) // per_level
    wrap_flags = jnp.logical_and(top_level, lev_window == levels // WIN_LEV - 1)
    contract_last = (((1,), (1,)), ((), ()))
    contract_first = (((0,), (0,)), ((), ()))
    grid_in = tokens.reshape(levels, extent, extent, model_width)
    grid_up = upstream.reshape(levels, extent, extent, model_width)
    paired = roll_local(
        jnp.concatenate([grid_in, grid_up], axis=-1), east_flag, north_flag, north_step
    )
    grid_in = paired[..., :model_width]
    grid_up = paired[..., model_width:]
    token_rows = grid_in.reshape(-1, model_width)
    upstream_rows = grid_up.reshape(-1, model_width)
    normalized, inverse = layer_stats(token_rows)
    hidden = normalized.astype(jnp.bfloat16)
    full_qkv, full_proj = (
        lax.all_gather(w_qkv, "tile", axis=0, tiled=True),
        lax.all_gather(w_proj, "tile", axis=0, tiled=True),
    )
    projected = jnp.dot(hidden, full_qkv, preferred_element_type=jnp.float32).astype(jnp.bfloat16)
    grid_qkv = projected.reshape(levels, extent, extent, 3 * model_width)
    windows_qkv = to_windows(grid_qkv)
    attended, prob, prob_low = attend_forward(windows_qkv, wrap_flags)
    grid_mixed = from_windows(attended, levels, extent)
    mixed_in = grid_mixed.reshape(-1, model_width)
    mixed_out = lax.dot_general(
        mixed_in, full_proj, contract_last, preferred_element_type=jnp.float32
    )
    back_mix = jnp.dot(upstream_rows, full_proj, preferred_element_type=jnp.float32)
    output_low = (token_rows.astype(jnp.float32) + mixed_out).astype(jnp.bfloat16)
    back_low = back_mix.astype(jnp.bfloat16)
    grid_back = back_low.reshape(levels, extent, extent, model_width)
    grad_windows = attend_backward(windows_qkv, to_windows(grid_back), prob, prob_low)
    grid_grad = from_windows(grad_windows, levels, extent)
    grad_qkv_tok = grid_grad.reshape(-1, 3 * model_width)
    grad_hidden = lax.dot_general(
        grad_qkv_tok, full_qkv, contract_last, preferred_element_type=jnp.float32
    )
    grad_low = norm_backward(upstream_rows, grad_hidden, normalized, inverse)
    grid_output = output_low.reshape(levels, extent, extent, model_width)
    grid_dx = grad_low.reshape(levels, extent, extent, model_width)
    paired = unroll_local(
        jnp.concatenate([grid_output, grid_dx], axis=-1), east_flag, north_flag, north_step
    )
    grid_output = paired[..., :model_width]
    grid_dx = paired[..., model_width:]
    columns = hidden
    share_qkv = lax.psum_scatter(
        lax.dot_general(
            columns, grad_qkv_tok, contract_first, preferred_element_type=jnp.float32
        ).astype(jnp.bfloat16),
        "tile",
        scatter_dimension=0,
        tiled=True,
    )
    columns = upstream_rows
    share_proj = lax.psum_scatter(
        lax.dot_general(
            columns, mixed_in, contract_first, preferred_element_type=jnp.float32
        ).astype(jnp.bfloat16),
        "tile",
        scatter_dimension=0,
        tiled=True,
    )
    grad_qkv, grad_proj = (
        lax.psum(share_qkv, ("rep", "lev")).astype(jnp.float32),
        lax.psum(share_proj, ("rep", "lev")).astype(jnp.float32),
    )
    return (grid_output.reshape(tokens.shape), grid_dx.reshape(tokens.shape), grad_qkv, grad_proj)


def solution(mesh):
    in_specs = (
        P("rep", "lev", "tile", None, None, None),
        P("tile", None),
        P("tile", None),
        P(),
        P("rep", "lev", "tile", None, None, None),
    )
    out_specs = (
        P("rep", "lev", "tile", None, None, None),
        P("rep", "lev", "tile", None, None, None),
        P("tile", None),
        P("tile", None),
    )
    return jax.shard_map(shards, mesh=mesh, in_specs=in_specs, out_specs=out_specs, check_vma=False)
```

profile of v0, /device:TPU:0, one launch (start us, length us, event | category | flops | bytes accessed | tf_op | source)
XLA Modules:
  0.0 227.7 jit_solution(8522655258842704439)
XLA Ops:
  7.2 0.0 all-gather.3.cloned.1.call-start
  7.2 0.7 all-gather.3.cloned.1.call-update
  7.9 0.0 all-gather.5.cloned.1.call-start
  8.0 1.4 fusion.34
  9.3 2.5 %collective-permute-start = (bf16[2,8,4,1536]{3,2,1,0:T(4,128)(2,1)S(1)}, bf16[2,8,4,1536]{3,2,1,0:T(4,128)(2,1)S(1)}, u32[]{:S(2)}, u32[]{:S(2)}) collective-permute-start(bf16[2,8,4,1536]{3,2,1,0:T(4,128)(2,1)S(1)} %get-tuple-element.22), channel_id=1, source_target_pairs={{0,3},{1,0},{2,1},{3,2},{4,7},{5,4},{6,5},{7,6},{8,11},{9,8},{10,9... | collective-permute-start | bytes 589832 | tf_op jit(solution)/shard_map/ppermute | solution.py:15
  11.8 0.6 constant_dynamic-slice_fusion
  13.1 1.9 collective-permute-done
  15.0 0.1 reverse_select_fusion.1
  15.1 0.2 fusion.33
  15.3 2.0 collective-permute-start.1
  17.3 0.0 all-gather.5.cloned.1.call-update
  17.3 0.0 reduce-scatter.5.cloned.1.call-start
  18.0 2.5 %collective-permute-done.1 = bf16[2,4,8,1536]{3,2,1,0:T(8,128)(2,1)S(1)} collective-permute-done((bf16[2,4,8,1536]{3,2,1,0:T(8,128)(2,1)S(1)}, bf16[2,4,8,1536]{3,2,1,0:T(8,128)(2,1)S(1)}, u32[]{:S(2)}, u32[]{:S(2)}) %collective-permute-start.1) | collective-permute-done | bytes 196640 | tf_op jit(solution)/shard_map/ppermute | solution.py:15
  20.5 0.3 rev.13
  20.9 3.7 %collective-permute-start.2 = (bf16[1,8,8,1536]{3,2,1,0:T(8,128)(2,1)S(1)}, bf16[1,8,8,1536]{3,2,1,0:T(8,128)(2,1)S(1)}, u32[]{:S(2)}, u32[]{:S(2)}) collective-permute-start(bf16[1,8,8,1536]{3,2,1,0:T(8,128)(2,1)S(1)} %get-tuple-element.18), channel_id=1, source_target_pairs={{0,12},{4,0},{8,4},{12,8},{1,13},{5,1},{9,5},{13,9},{2,14},{6,2},{... | collective-permute-start | bytes 589832 | tf_op jit(solution)/shard_map/ppermute | solution.py:15
  24.7 0.1 or_convert_fusion
  24.8 4.9 %collective-permute-done.2 = bf16[1,8,8,1536]{3,2,1,0:T(8,128)(2,1)S(1)} collective-permute-done((bf16[1,8,8,1536]{3,2,1,0:T(8,128)(2,1)S(1)}, bf16[1,8,8,1536]{3,2,1,0:T(8,128)(2,1)S(1)}, u32[]{:S(2)}, u32[]{:S(2)}) %collective-permute-start.2) | collective-permute-done | bytes 196640 | tf_op jit(solution)/shard_map/ppermute | solution.py:15
  29.7 0.1 convert_reduce_fusion
  29.8 0.2 multiply_reduce_fusion.2
  30.0 0.1 div.36
  30.1 0.1 rsqrt.12
  30.2 0.1 fusion.27
  30.3 12.7 %all-gather.3.cloned.1.call-done = bf16[768,2304]{1,0:T(8,128)(2,1)} async-done(((bf16[192,2304]{1,0:T(8,128)(2,1)}), bf16[768,2304]{1,0:T(8,128)(2,1)}) %all-gather.3.cloned.1.call-update) | async-done | bytes 3538960 | tf_op jit(solution)/shard_map/all_gather | solution.py:178
  43.0 2.7 %fusion.1 = bf16[1,128,2304]{2,1,0:T(8,128)(2,1)S(1)} fusion(bf16[128,768]{1,0:T(8,128)(2,1)S(1)} %fusion.27, bf16[768,2304]{1,0:T(8,128)(2,1)} %all-gather.3.cloned.1.call-done), kind=kOutput, calls=%fused_computation.3 | convolution fusion | flops 453279744 | bytes 4325376 | tf_op jit(solution)/shard_map/dot_general | solution.py:181
  45.8 0.2 copy.21
  45.9 0.2 copy.23
  46.1 0.2 copy.22
  46.3 0.5 exponential_multiply_fusion
  46.7 0.4 convolution_convert_fusion.5
  47.1 1.6 convolution_convert_fusion.2
  48.7 0.0 reduce-scatter.3.cloned.1.call-start
  48.8 13.5 %all-gather.5.cloned.1.call-done = bf16[768,768]{1,0:T(8,128)(2,1)} async-done(((bf16[192,768]{1,0:T(8,128)(2,1)}), bf16[768,768]{1,0:T(8,128)(2,1)}) %all-gather.5.cloned.1.call-update) | async-done | bytes 1179664 | tf_op jit(solution)/shard_map/all_gather | solution.py:179
  62.2 1.6 convolution_convert_fusion.3
  63.8 0.2 copy.25
  64.0 0.5 convolution_convert_fusion.4
  64.6 0.4 fusion.47
  65.0 0.5 copy-done.2
  65.5 1.8 fusion.19
  67.2 2.5 %fusion.11 = bf16[24,32,128]{2,1,0:T(8,128)(2,1)S(1)} fusion(bf16[128,24,32]{0,2,1:T(8,128)(2,1)S(1)} %bitcast.82, f32[24,128,128]{1,2,0:T(8,128)} %fusion.19, f32[24,128,128]{1,2,0:T(8,128)S(1)} %fusion.47), kind=kOutput, calls=%fused_computation.12 | convolution fusion | flops 27233408 | bytes 3538944 | tf_op jit(solution)/shard_map/whqk,wkhd->wqhd/dot_general | solution.py:131
  69.7 2.6 %fusion.14 = bf16[24,32,128]{2,1,0:T(8,128)(2,1)S(1)} fusion(bf16[128,24,32]{0,2,1:T(8,128)(2,1)S(1)} %bitcast.85, f32[24,128,128]{1,2,0:T(8,128)} %fusion.19, f32[24,128,128]{1,2,0:T(8,128)S(1)} %fusion.47), kind=kOutput, calls=%fused_computation.13 | convolution fusion | flops 27233408 | bytes 3538944 | tf_op jit(solution)/shard_map/whqk,wqhd->wkhd/dot_general | solution.py:134
  72.3 0.0 copy-start.5
  72.4 2.9 %convolution_convert_fusion = bf16[768,2304]{1,0:T(8,128)(2,1)} fusion(bf16[128,768]{1,0:T(8,128)(2,1)S(1)} %fusion.27, bf16[128,768]{0,1:T(8,128)(2,1)S(1)} %bitcast.92, bf16[128,768]{0,1:T(8,128)(2,1)S(1)} %bitcast.96, bf16[128,768]{0,1:T(8,128)(2,1)S(1)} %bitcast.94), kind=kOutput, calls=%fused_computation.1 | convolution fusion | flops 456523776 | bytes 4325376 | tf_op jit(solution)/shard_map/dot_general | solution.py:210
  75.3 0.0 reduce-scatter.3.cloned.1.call-update
  75.3 0.0 all-reduce.3.cloned.1.call-start
  75.4 0.8 copy-done.4
  76.2 0.1 copy-done.6
  76.3 3.4 %fusion.44 = (f32[128]{0:T(128)S(1)}, f32[128]{0:T(128)S(1)}, f32[128,768]{1,0:T(8,128)S(1)}) fusion(f32[128]{0:T(128)S(1)} %rsqrt.12, f32[128]{0:T(128)S(1)} %div.36, bf16[2,8,8,768]{3,2,1,0:T(8,128)(2,1)S(1)} %get-tuple-element.9, bf16[768,2304]{1,0:T(8,128)(2,1)} %all-gather.3.cloned.1.call-done, bf16[128,768]{0,1:T(8,128)(2,1)S(1)} %bitcast.93, ...), kind=kOutput, calls=%fused_computation.85 | convolution fusion | flops 455343872 | bytes 4720640 | tf_op jit(solution)/shard_map/dot_general | solution.py:197
  79.8 0.2 add_convert_fusion
  80.0 0.5 fusion.17
  80.5 1.6 collective-permute-start.3
  82.1 7.3 %collective-permute-done.3 = bf16[1,8,8,1536]{3,2,1,0:T(8,128)(2,1)S(1)} collective-permute-done((bf16[1,8,8,1536]{3,2,1,0:T(8,128)(2,1)S(1)}, bf16[1,8,8,1536]{3,2,1,0:T(8,128)(2,1)S(1)}, u32[]{:S(2)}, u32[]{:S(2)}) %collective-permute-start.3) | collective-permute-done | bytes 196640 | tf_op jit(solution)/shard_map/ppermute | solution.py:15
  89.5 0.3 rev.14
  89.9 0.1 collective-permute-start.4
  89.9 0.5 reduce-scatter.5.cloned.1.call-done
  90.4 42.9 %reduce-scatter.3.cloned.1.call-done = bf16[192,2304]{1,0:T(8,128)(2,1)} async-done(((bf16[768,2304]{1,0:T(8,128)(2,1)}), bf16[192,2304]{1,0:T(8,128)(2,1)}) %reduce-scatter.3.cloned.1.call-update) | async-done | bytes 884752 | tf_op jit(solution)/shard_map/reduce_scatter | solution.py:209
  133.3 0.2 fusion.29
  133.5 0.1 reverse_select_fusion
  133.6 0.1 collective-permute-start.5
  133.6 5.1 %collective-permute-done.5 = bf16[2,8,4,1536]{3,2,1,0:T(4,128)(2,1)S(1)} collective-permute-done((bf16[2,8,4,1536]{3,2,1,0:T(4,128)(2,1)S(1)}, bf16[2,8,4,1536]{3,2,1,0:T(4,128)(2,1)S(1)}, u32[]{:S(2)}, u32[]{:S(2)}) %collective-permute-start.5) | collective-permute-done | bytes 196640 | tf_op jit(solution)/shard_map/ppermute | solution.py:15
  138.7 0.2 fusion.22
  138.9 0.8 slice_bitcast_fusion
  139.7 77.2 %all-reduce.3.cloned.1.call-done = (bf16[192,2304]{1,0:T(8,128)(2,1)}, bf16[192,768]{1,0:T(8,128)(2,1)}) async-done(((bf16[192,2304]{1,0:T(8,128)(2,1)}, bf16[192,768]{1,0:T(8,128)(2,1)}), (bf16[192,2304]{1,0:T(8,128)(2,1)}, bf16[192,768]{1,0:T(8,128)(2,1)})) %all-reduce.3.cloned.1.call-update) | async-done | bytes 1179664 | tf_op jit(solution)/shard_map/psum | solution.py:227
  216.9 1.8 convert_element_type.88
  218.7 2.5 %convert_element_type.86 = f32[192,2304]{1,0:T(8,128)} convert(bf16[192,2304]{1,0:T(8,128)(2,1)} %get-tuple-element.6) | non-fusion elementwise | flops 442368 | bytes 2654208 | tf_op jit(solution)/shard_map/convert_element_type | solution.py:227
  (27 shorter events, 0.3 us)
Async XLA Ops:
  7.2 4.7 %copy-start.7 = (s32[4,2]{0,1:T(2,128)S(1)}, s32[4,2]{0,1:T(2,128)}, u32[]{:S(2)}) copy-start(s32[4,2]{0,1:T(2,128)} %param.8) | copy-start | bytes 100
  7.2 35.9 %all-gather.3.cloned.1.call-start = ((), (), s32[]{:S(2)}) async-start(), calls=%async_computation.2 | async-start | bytes 4423680 | tf_op jit(solution)/shard_map/all_gather | solution.py:178
  7.9 54.3 %all-gather.5.cloned.1.call-start = ((), (), s32[]{:S(2)}) async-start(), calls=%async_computation.3 | async-start | bytes 1474560 | tf_op jit(solution)/shard_map/all_gather | solution.py:179
  9.3 5.7 %collective-permute-start = (bf16[2,8,4,1536]{3,2,1,0:T(4,128)(2,1)S(1)}, bf16[2,8,4,1536]{3,2,1,0:T(4,128)(2,1)S(1)}, u32[]{:S(2)}, u32[]{:S(2)}) collective-permute-start(bf16[2,8,4,1536]{3,2,1,0:T(4,128)(2,1)S(1)} %get-tuple-element.22), channel_id=1, source_target_pairs={{0,3},{1,0},{2,1},{3,2},{4,7},{5,4},{6,5},{7,6},{8,11},{9,8},{10,9... | collective-permute-start | bytes 589832 | tf_op jit(solution)/shard_map/ppermute | solution.py:15
  15.3 5.2 %collective-permute-start.1 = (bf16[2,4,8,1536]{3,2,1,0:T(8,128)(2,1)S(1)}, bf16[2,4,8,1536]{3,2,1,0:T(8,128)(2,1)S(1)}, u32[]{:S(2)}, u32[]{:S(2)}) collective-permute-start(bf16[2,4,8,1536]{3,2,1,0:T(8,128)(2,1)S(1)} %get-tuple-element.20), channel_id=1, source_target_pairs={{0,3},{1,0},{2,1},{3,2},{4,7},{5,4},{6,5},{7,6},{8,11},{9,8},{10,9... | collective-permute-start | bytes 589832 | tf_op jit(solution)/shard_map/ppermute | solution.py:15
  17.3 73.1 %reduce-scatter.5.cloned.1.call-start = ((), (), s32[]{:S(2)}) async-start(), calls=%async_computation.5 | async-start | bytes 1474560 | tf_op jit(solution)/shard_map/reduce_scatter | solution.py:218
  20.9 8.7 %collective-permute-start.2 = (bf16[1,8,8,1536]{3,2,1,0:T(8,128)(2,1)S(1)}, bf16[1,8,8,1536]{3,2,1,0:T(8,128)(2,1)S(1)}, u32[]{:S(2)}, u32[]{:S(2)}) collective-permute-start(bf16[1,8,8,1536]{3,2,1,0:T(8,128)(2,1)S(1)} %get-tuple-element.18), channel_id=1, source_target_pairs={{0,12},{4,0},{8,4},{12,8},{1,13},{5,1},{9,5},{13,9},{2,14},{6,2},{... | collective-permute-start | bytes 589832 | tf_op jit(solution)/shard_map/ppermute | solution.py:15
  24.7 21.5 %copy-start.1 = (f32[128,128]{0,1:T(8,128)}, f32[128,128]{0,1:T(8,128)S(1)}, u32[]{:S(2)}) copy-start(f32[128,128]{0,1:T(8,128)S(1)} %or_convert_fusion) | copy-start | bytes 196612
  48.7 84.6 %reduce-scatter.3.cloned.1.call-start = ((), (), s32[]{:S(2)}) async-start(), calls=%async_computation.4 | async-start | bytes 4423680 | tf_op jit(solution)/shard_map/reduce_scatter | solution.py:209
  64.5 7.8 %copy-start.3 = (bf16[24,32,128]{2,1,0:T(8,128)(2,1)}, bf16[24,32,128]{2,1,0:T(8,128)(2,1)S(1)}, u32[]{:S(2)}) copy-start(bf16[24,32,128]{2,1,0:T(8,128)(2,1)S(1)} %convolution_convert_fusion.4) | copy-start | bytes 589828
  64.6 0.9 copy-start.2
  72.3 3.0 %copy-start.5 = (bf16[24,32,128]{2,1,0:T(8,128)(2,1)}, bf16[24,32,128]{2,1,0:T(8,128)(2,1)S(1)}, u32[]{:S(2)}) copy-start(bf16[24,32,128]{2,1,0:T(8,128)(2,1)S(1)} %fusion.14) | copy-start | bytes 589828
  75.3 0.9 copy-start.4
  75.3 1.0 copy-start.6
  75.3 4.6 %copy-start = (bf16[768,768]{1,0:T(8,128)(2,1)S(1)}, bf16[768,768]{1,0:T(8,128)(2,1)}, u32[]{:S(2)}) copy-start(bf16[768,768]{1,0:T(8,128)(2,1)} %all-gather.5.cloned.1.call-done) | copy-start | bytes 3538948
  75.3 141.6 %all-reduce.3.cloned.1.call-start = ((), (), s32[]{:S(2)}) async-start(), calls=%async_computation.6 | async-start | bytes 2359296 | tf_op jit(solution)/shard_map/psum | solution.py:227
  80.5 8.9 %collective-permute-start.3 = (bf16[1,8,8,1536]{3,2,1,0:T(8,128)(2,1)S(1)}, bf16[1,8,8,1536]{3,2,1,0:T(8,128)(2,1)S(1)}, u32[]{:S(2)}, u32[]{:S(2)}) collective-permute-start(bf16[1,8,8,1536]{3,2,1,0:T(8,128)(2,1)S(1)} %fusion.30), channel_id=1, source_target_pairs={{0,4},{4,8},{8,12},{12,0},{1,5},{5,9},{9,13},{13,1},{2,6},{6,10},{... | collective-permute-start | bytes 589832 | tf_op jit(solution)/shard_map/ppermute | solution.py:15
  89.9 43.4 %collective-permute-start.4 = (bf16[2,4,8,1536]{3,2,1,0:T(8,128)(2,1)S(1)}, bf16[2,4,8,1536]{3,2,1,0:T(8,128)(2,1)S(1)}, u32[]{:S(2)}, u32[]{:S(2)}) collective-permute-start(bf16[2,4,8,1536]{3,2,1,0:T(8,128)(2,1)S(1)} %get-tuple-element.15), channel_id=1, source_target_pairs={{0,1},{1,2},{2,3},{3,0},{4,5},{5,6},{6,7},{7,4},{8,9},{9,10},{10,1... | collective-permute-start | bytes 589832 | tf_op jit(solution)/shard_map/ppermute | solution.py:15
  133.6 5.1 %collective-permute-start.5 = (bf16[2,8,4,1536]{3,2,1,0:T(4,128)(2,1)S(1)}, bf16[2,8,4,1536]{3,2,1,0:T(4,128)(2,1)S(1)}, u32[]{:S(2)}, u32[]{:S(2)}) collective-permute-start(bf16[2,8,4,1536]{3,2,1,0:T(4,128)(2,1)S(1)} %reverse_select_fusion), channel_id=1, source_target_pairs={{0,1},{1,2},{2,3},{3,0},{4,5},{5,6},{6,7},{7,4},{8,9},{9,10},{10,1... | collective-permute-start | bytes 589832 | tf_op jit(solution)/shard_map/ppermute | solution.py:15
Sparse Core Ops, SparseCore 0:
  9.5 33.4 all-gather.2
  44.6 17.5 all-gather.4
  64.8 25.5 reduce-scatter.4
  92.8 40.3 reduce-scatter.2
  136.7 80.2 all-reduce.2
where the time goes:
time: 228 us
  waiting for transfers between devices  169 us (74%)
  matrix products  21.4 us (9%)
  between operations  15.4 us (7%)
  starting transfers between devices  10.1 us (4%)
  other arithmetic  7.28 us (3%)
  local copies, waits for them, and re-layouts  4.35 us (2%)
    psum x1, waiting for transfers between devices, shards(): lax.psum(share_qkv, ('rep', 'lev')).astype(jnp.float32)  77.2 us
    reduce_scatter x1, waiting for transfers between devices, shards(): lax.psum_scatter(lax.dot_general(columns, grad_qkv_tok, contract_first, p...  42.9 us
    ppermute x6, waiting for transfers between devices, shifted(): return lax.ppermute(value, axis, pairs)  21.8 us
    all_gather x1, waiting for transfers between devices, shards(): lax.all_gather(w_proj, 'tile', axis=0, tiled=True)  13.5 us
    all_gather x1, waiting for transfers between devices, shards(): lax.all_gather(w_qkv, 'tile', axis=0, tiled=True)  12.7 us
    ppermute x6, starting transfers between devices, shifted(): return lax.ppermute(value, axis, pairs)  9.89 us
  transfers between devices with their start and end apart: 11, of which 10 were waited for; matrix products, arithmetic and copies ran while one was open for 12% of the time, Pallas kernels for 0%

commit v1 on v0

--- a/solution.py
+++ b/solution.py
@@ -224,7 +224,7 @@
         tiled=True,
     )
     grad_qkv, grad_proj = (
-        lax.psum(share_qkv, ("rep", "lev")).astype(jnp.float32),
+        lax.psum(lax.psum(share_qkv, "lev"), "rep").astype(jnp.float32),
         lax.psum(share_proj, ("rep", "lev")).astype(jnp.float32),
     )
     return (grid_output.reshape(tokens.shape), grid_dx.reshape(tokens.shape), grad_qkv, grad_proj)

time: 228 us -> 320 us (1.40)
  waiting for transfers between devices: 169 us -> 260 us
    psum x1 -> x3, waiting for transfers between devices: 77.2 us -> 152 us  [the longest x1 67.4 us: shards(): lax.psum(share_proj, ('rep', 'lev')).astype(jnp.float32)]
    reduce_scatter x1, waiting for transfers between devices: 0.48 us -> 28 us  [shards(): lax.psum_scatter(lax.dot_general(columns, mixed_in, contract_first, prefe...]
    all_gather x1, waiting for transfers between devices: 12.7 us -> 29.3 us  [shards(): lax.all_gather(w_qkv, 'tile', axis=0, tiled=True)]
    all_gather x1, waiting for transfers between devices: 13.5 us -> 0.02 us  [shards(): lax.all_gather(w_proj, 'tile', axis=0, tiled=True)]
    reduce_scatter x1, waiting for transfers between devices: 42.9 us -> 32.7 us  [shards(): lax.psum_scatter(lax.dot_general(columns, grad_qkv_tok, contract_first, p...]
    ppermute x6, waiting for transfers between devices: 21.8 us -> 16 us  [shifted(): return lax.ppermute(value, axis, pairs)]
  transfers between devices with their start and end apart: 11 -> 13, of which waited for: 10 -> 10; matrix products, arithmetic and copies ran while one was open for 12% -> 5% of each run, Pallas kernels for 0% -> 0%
where the time goes in v1:
time: 320 us
  waiting for transfers between devices  260 us (81%)
  matrix products  24.3 us (8%)
  between operations  15.7 us (5%)
  starting transfers between devices  10.1 us (3%)
  other arithmetic  7.27 us (2%)
    psum x1, waiting for transfers between devices, shards(): lax.psum(share_proj, ('rep', 'lev')).astype(jnp.float32)  67.4 us
    psum x1, waiting for transfers between devices, shards(): lax.psum(share_qkv, 'lev')  48.8 us
    psum x1, waiting for transfers between devices, shards(): lax.psum(lax.psum(share_qkv, 'lev'), 'rep').astype(jnp.float32)  36.1 us
    reduce_scatter x1, waiting for transfers between devices, shards(): lax.psum_scatter(lax.dot_general(columns, grad_qkv_tok, contract_first, p...  32.7 us
    all_gather x1, waiting for transfers between devices, shards(): lax.all_gather(w_qkv, 'tile', axis=0, tiled=True)  29.3 us
    reduce_scatter x1, waiting for transfers between devices, shards(): lax.psum_scatter(lax.dot_general(columns, mixed_in, contract_first, prefe...  28 us
    ppermute x6, waiting for transfers between devices, shifted(): return lax.ppermute(value, axis, pairs)  16 us
    ppermute x6, starting transfers between devices, shifted(): return lax.ppermute(value, axis, pairs)  9.78 us
  transfers between devices with their start and end apart: 13, of which 10 were waited for; matrix products, arithmetic and copies ran while one was open for 5% of the time, Pallas kernels for 0%

profile of v1, /device:TPU:0, one launch (start us, length us, event | category | flops | bytes accessed | tf_op | source)
XLA Modules:
  0.0 320.0 jit_solution(7504188396328956222)
XLA Ops:
  7.2 0.0 all-gather.5.cloned.1.call-start
  7.2 0.7 all-gather.5.cloned.1.call-update
  7.9 0.0 all-gather.3.cloned.1.call-start
  8.0 0.7 all-gather.3.cloned.1.call-update
  8.7 0.0 reduce-scatter.3.cloned.1.call-start
  8.7 1.4 fusion.34
  10.1 2.5 collective-permute-start
  12.6 0.6 constant_dynamic-slice_fusion
  13.8 1.9 collective-permute-done
  15.8 0.1 reverse_select_fusion.1
  15.8 0.2 fusion.33
  16.0 2.0 collective-permute-start.1
  18.7 5.3 %collective-permute-done.1 = bf16[2,4,8,1536]{3,2,1,0:T(8,128)(2,1)S(1)} collective-permute-done((bf16[2,4,8,1536]{3,2,1,0:T(8,128)(2,1)S(1)}, bf16[2,4,8,1536]{3,2,1,0:T(8,128)(2,1)S(1)}, u32[]{:S(2)}, u32[]{:S(2)}) %collective-permute-start.1) | collective-permute-done | bytes 196640 | tf_op jit(solution)/shard_map/ppermute | solution.py:15
  24.0 0.3 rev.13
  24.4 3.7 %collective-permute-start.2 = (bf16[1,8,8,1536]{3,2,1,0:T(8,128)(2,1)S(1)}, bf16[1,8,8,1536]{3,2,1,0:T(8,128)(2,1)S(1)}, u32[]{:S(2)}, u32[]{:S(2)}) collective-permute-start(bf16[1,8,8,1536]{3,2,1,0:T(8,128)(2,1)S(1)} %get-tuple-element.16), channel_id=1, source_target_pairs={{0,12},{4,0},{8,4},{12,8},{1,13},{5,1},{9,5},{13,9},{2,14},{6,2},{... | collective-permute-start | bytes 589832 | tf_op jit(solution)/shard_map/ppermute | solution.py:15
  28.1 0.1 or_convert_fusion
  28.2 3.7 %collective-permute-done.2 = bf16[1,8,8,1536]{3,2,1,0:T(8,128)(2,1)S(1)} collective-permute-done((bf16[1,8,8,1536]{3,2,1,0:T(8,128)(2,1)S(1)}, bf16[1,8,8,1536]{3,2,1,0:T(8,128)(2,1)S(1)}, u32[]{:S(2)}, u32[]{:S(2)}) %collective-permute-start.2) | collective-permute-done | bytes 196640 | tf_op jit(solution)/shard_map/ppermute | solution.py:15
  31.8 0.1 convert_reduce_fusion
  31.9 0.1 div.36
  32.0 0.2 multiply_reduce_fusion.2
  32.2 0.1 rsqrt.12
  32.3 0.1 fusion.27
  32.5 0.0 all-gather.5.cloned.1.call-done
  32.5 1.6 convolution_convert_fusion.3
  34.1 0.2 copy.25
  34.3 29.3 %all-gather.3.cloned.1.call-done = bf16[768,2304]{1,0:T(8,128)(2,1)} async-done(((bf16[192,2304]{1,0:T(8,128)(2,1)}), bf16[768,2304]{1,0:T(8,128)(2,1)}) %all-gather.3.cloned.1.call-update) | async-done | bytes 3538960 | tf_op jit(solution)/shard_map/all_gather | solution.py:178
  63.6 2.6 fusion.1
  66.3 0.2 copy.23
  66.4 0.2 copy.22
  66.6 1.8 fusion.19
  68.4 0.5 exponential_multiply_fusion
  68.8 0.2 copy.21
  69.0 1.6 fusion.47
  70.6 3.4 %fusion.11 = bf16[24,32,128]{2,1,0:T(8,128)(2,1)S(1)} fusion(bf16[128,24,32]{0,2,1:T(8,128)(2,1)S(1)} %bitcast.86, f32[24,128,128]{1,2,0:T(8,128)} %fusion.19, f32[24,128,128]{1,2,0:T(8,128)} %fusion.47), kind=kOutput, calls=%fused_computation.12 | convolution fusion | flops 27233408 | bytes 3538944 | tf_op jit(solution)/shard_map/whqk,wkhd->wqhd/dot_general | solution.py:131
  74.0 3.5 %fusion.14 = bf16[24,32,128]{2,1,0:T(8,128)(2,1)S(1)} fusion(bf16[128,24,32]{0,2,1:T(8,128)(2,1)S(1)} %bitcast.89, f32[24,128,128]{1,2,0:T(8,128)} %fusion.19, f32[24,128,128]{1,2,0:T(8,128)} %fusion.47), kind=kOutput, calls=%fused_computation.13 | convolution fusion | flops 27233408 | bytes 3538944 | tf_op jit(solution)/shard_map/whqk,wqhd->wkhd/dot_general | solution.py:134
  77.5 0.6 convolution_convert_fusion.4
  78.0 2.9 convolution_convert_fusion
  81.0 0.0 reduce-scatter.3.cloned.1.call-update
  81.0 0.0 reduce-scatter.5.cloned.1.call-start
  81.0 0.3 convolution_convert_fusion.5
  81.4 1.5 convolution_convert_fusion.2
  82.9 0.0 reduce-scatter.5.cloned.1.call-update
  82.9 0.0 all-reduce.4.cloned.1.call-start
  83.0 3.5 %fusion.44 = (f32[128]{0:T(128)S(1)}, f32[128]{0:T(128)S(1)}, f32[128,768]{1,0:T(8,128)S(1)}) fusion(f32[128]{0:T(128)S(1)} %rsqrt.12, f32[128]{0:T(128)S(1)} %div.36, bf16[2,8,8,768]{3,2,1,0:T(8,128)(2,1)S(1)} %get-tuple-element.7, bf16[768,2304]{1,0:T(8,128)(2,1)} %all-gather.3.cloned.1.call-done, bf16[128,768]{0,1:T(8,128)(2,1)S(1)} %bitcast.97, ...), kind=kOutput, calls=%fused_computation.85 | convolution fusion | flops 455343872 | bytes 4720640 | tf_op jit(solution)/shard_map/dot_general | solution.py:197
  86.5 0.2 add_convert_fusion
  86.7 0.5 fusion.17
  87.3 1.5 collective-permute-start.3
  88.8 32.7 %reduce-scatter.3.cloned.1.call-done = bf16[192,2304]{1,0:T(8,128)(2,1)} async-done(((bf16[768,2304]{1,0:T(8,128)(2,1)}), bf16[192,2304]{1,0:T(8,128)(2,1)}) %reduce-scatter.3.cloned.1.call-update) | async-done | bytes 884752 | tf_op jit(solution)/shard_map/reduce_scatter | solution.py:209
  121.5 0.0 all-reduce.8.cloned.1.call-start
  121.6 0.3 rev.14
  122.0 0.1 collective-permute-start.4
  122.1 28.0 %reduce-scatter.5.cloned.1.call-done = bf16[192,768]{1,0:T(8,128)(2,1)} async-done(((bf16[768,768]{1,0:T(8,128)(2,1)}), bf16[192,768]{1,0:T(8,128)(2,1)}) %reduce-scatter.5.cloned.1.call-update) | async-done | bytes 294928 | tf_op jit(solution)/shard_map/reduce_scatter | solution.py:218
  150.1 0.0 all-reduce.6.cloned.1.call-start
  150.2 0.2 fusion.29
  150.4 48.8 %all-reduce.4.cloned.1.call-done = bf16[192,2304]{1,0:T(8,128)(2,1)} async-done(((bf16[192,2304]{1,0:T(8,128)(2,1)}), bf16[192,2304]{1,0:T(8,128)(2,1)}) %all-reduce.4.cloned.1.call-update) | async-done | bytes 884752 | tf_op jit(solution)/shard_map/psum | solution.py:227
  199.2 0.1 reverse_select_fusion
  199.3 0.1 collective-permute-start.5
  199.4 5.1 %collective-permute-done.5 = bf16[2,8,4,1536]{3,2,1,0:T(4,128)(2,1)S(1)} collective-permute-done((bf16[2,8,4,1536]{3,2,1,0:T(4,128)(2,1)S(1)}, bf16[2,8,4,1536]{3,2,1,0:T(4,128)(2,1)S(1)}, u32[]{:S(2)}, u32[]{:S(2)}) %collective-permute-start.5) | collective-permute-done | bytes 196640 | tf_op jit(solution)/shard_map/ppermute | solution.py:15
  204.4 0.2 fusion.22
  204.6 0.8 slice_bitcast_fusion
  205.4 67.4 %all-reduce.8.cloned.1.call-done = bf16[192,768]{1,0:T(8,128)(2,1)} async-done(((bf16[192,768]{1,0:T(8,128)(2,1)}), bf16[192,768]{1,0:T(8,128)(2,1)}) %all-reduce.8.cloned.1.call-update) | async-done | bytes 294928 | tf_op jit(solution)/shard_map/psum | solution.py:228
  272.8 1.8 convert_element_type.88
  274.6 36.1 %all-reduce.6.cloned.1.call-done = bf16[192,2304]{1,0:T(8,128)(2,1)} async-done(((bf16[192,2304]{1,0:T(8,128)(2,1)}), bf16[192,2304]{1,0:T(8,128)(2,1)}) %all-reduce.6.cloned.1.call-update) | async-done | bytes 884752 | tf_op jit(solution)/shard_map/psum | solution.py:227
  310.7 2.5 convert_element_type.86
  (21 shorter events, 0.3 us)
Async XLA Ops:
  7.2 5.4 %copy-start.1 = (s32[4,2]{0,1:T(2,128)S(1)}, s32[4,2]{0,1:T(2,128)}, u32[]{:S(2)}) copy-start(s32[4,2]{0,1:T(2,128)} %param.8) | copy-start | bytes 100
  7.2 25.3 %all-gather.5.cloned.1.call-start = ((), (), s32[]{:S(2)}) async-start(), calls=%async_computation.3 | async-start | bytes 1474560 | tf_op jit(solution)/shard_map/all_gather | solution.py:179
  7.9 55.6 %all-gather.3.cloned.1.call-start = ((), (), s32[]{:S(2)}) async-start(), calls=%async_computation.2 | async-start | bytes 4423680 | tf_op jit(solution)/shard_map/all_gather | solution.py:178
  8.7 112.8 %reduce-scatter.3.cloned.1.call-start = ((), (), s32[]{:S(2)}) async-start(), calls=%async_computation.4 | async-start | bytes 4423680 | tf_op jit(solution)/shard_map/reduce_scatter | solution.py:209
  10.1 5.7 %collective-permute-start = (bf16[2,8,4,1536]{3,2,1,0:T(4,128)(2,1)S(1)}, bf16[2,8,4,1536]{3,2,1,0:T(4,128)(2,1)S(1)}, u32[]{:S(2)}, u32[]{:S(2)}) collective-permute-start(bf16[2,8,4,1536]{3,2,1,0:T(4,128)(2,1)S(1)} %get-tuple-element.20), channel_id=1, source_target_pairs={{0,3},{1,0},{2,1},{3,2},{4,7},{5,4},{6,5},{7,6},{8,11},{9,8},{10,9... | collective-permute-start | bytes 589832 | tf_op jit(solution)/shard_map/ppermute | solution.py:15
  16.0 7.9 %collective-permute-start.1 = (bf16[2,4,8,1536]{3,2,1,0:T(8,128)(2,1)S(1)}, bf16[2,4,8,1536]{3,2,1,0:T(8,128)(2,1)S(1)}, u32[]{:S(2)}, u32[]{:S(2)}) collective-permute-start(bf16[2,4,8,1536]{3,2,1,0:T(8,128)(2,1)S(1)} %get-tuple-element.18), channel_id=1, source_target_pairs={{0,3},{1,0},{2,1},{3,2},{4,7},{5,4},{6,5},{7,6},{8,11},{9,8},{10,9... | collective-permute-start | bytes 589832 | tf_op jit(solution)/shard_map/ppermute | solution.py:15
  24.4 7.4 %collective-permute-start.2 = (bf16[1,8,8,1536]{3,2,1,0:T(8,128)(2,1)S(1)}, bf16[1,8,8,1536]{3,2,1,0:T(8,128)(2,1)S(1)}, u32[]{:S(2)}, u32[]{:S(2)}) collective-permute-start(bf16[1,8,8,1536]{3,2,1,0:T(8,128)(2,1)S(1)} %get-tuple-element.16), channel_id=1, source_target_pairs={{0,12},{4,0},{8,4},{12,8},{1,13},{5,1},{9,5},{13,9},{2,14},{6,2},{... | collective-permute-start | bytes 589832 | tf_op jit(solution)/shard_map/ppermute | solution.py:15
  81.0 69.1 %reduce-scatter.5.cloned.1.call-start = ((), (), s32[]{:S(2)}) async-start(), calls=%async_computation.7 | async-start | bytes 1474560 | tf_op jit(solution)/shard_map/reduce_scatter | solution.py:218
  82.9 3.8 %copy-start = (bf16[768,768]{1,0:T(8,128)(2,1)S(1)}, bf16[768,768]{1,0:T(8,128)(2,1)}, u32[]{:S(2)}) copy-start(bf16[768,768]{1,0:T(8,128)(2,1)} %all-gather.5.cloned.1.call-done) | copy-start | bytes 3538948
  82.9 116.2 %all-reduce.4.cloned.1.call-start = ((), (), s32[]{:S(2)}) async-start(), calls=%async_computation.5 | async-start | bytes 1769472 | tf_op jit(solution)/shard_map/psum | solution.py:227
  87.3 34.3 %collective-permute-start.3 = (bf16[1,8,8,1536]{3,2,1,0:T(8,128)(2,1)S(1)}, bf16[1,8,8,1536]{3,2,1,0:T(8,128)(2,1)S(1)}, u32[]{:S(2)}, u32[]{:S(2)}) collective-permute-start(bf16[1,8,8,1536]{3,2,1,0:T(8,128)(2,1)S(1)} %fusion.30), channel_id=1, source_target_pairs={{0,4},{4,8},{8,12},{12,0},{1,5},{5,9},{9,13},{13,1},{2,6},{6,10},{... | collective-permute-start | bytes 589832 | tf_op jit(solution)/shard_map/ppermute | solution.py:15
  121.5 151.2 %all-reduce.8.cloned.1.call-start = ((), (), s32[]{:S(2)}) async-start(), calls=%async_computation.8 | async-start | bytes 589824 | tf_op jit(solution)/shard_map/psum | solution.py:228
  122.0 28.2 %collective-permute-start.4 = (bf16[2,4,8,1536]{3,2,1,0:T(8,128)(2,1)S(1)}, bf16[2,4,8,1536]{3,2,1,0:T(8,128)(2,1)S(1)}, u32[]{:S(2)}, u32[]{:S(2)}) collective-permute-start(bf16[2,4,8,1536]{3,2,1,0:T(8,128)(2,1)S(1)} %get-tuple-element.13), channel_id=1, source_target_pairs={{0,1},{1,2},{2,3},{3,0},{4,5},{5,6},{6,7},{7,4},{8,9},{9,10},{10,1... | collective-permute-start | bytes 589832 | tf_op jit(solution)/shard_map/ppermute | solution.py:15
  150.1 160.5 %all-reduce.6.cloned.1.call-start = ((), (), s32[]{:S(2)}) async-start(), calls=%async_computation.6 | async-start | bytes 1769472 | tf_op jit(solution)/shard_map/psum | solution.py:227
  199.3 5.1 %collective-permute-start.5 = (bf16[2,8,4,1536]{3,2,1,0:T(4,128)(2,1)S(1)}, bf16[2,8,4,1536]{3,2,1,0:T(4,128)(2,1)S(1)}, u32[]{:S(2)}, u32[]{:S(2)}) collective-permute-start(bf16[2,8,4,1536]{3,2,1,0:T(4,128)(2,1)S(1)} %reverse_select_fusion), channel_id=1, source_target_pairs={{0,1},{1,2},{2,3},{3,0},{4,5},{5,6},{6,7},{7,4},{8,9},{9,10},{10,1... | collective-permute-start | bytes 589832 | tf_op jit(solution)/shard_map/ppermute | solution.py:15
Sparse Core Ops, SparseCore 0:
  9.5 20.4 all-gather.4
  31.6 31.9 all-gather.2
  81.1 40.3 reduce-scatter.2
  124.5 25.5 reduce-scatter.4
  152.3 46.7 all-reduce.3
  202.4 70.3 all-reduce.7
  275.1 35.5 all-reduce.5
